TPU v7x, 128 devices: a whole 4x4x4 slice. The times are simulated.
128 devices in a mesh: row: 8 (over z, y_hi), col: 16 (over y_lo, x, core).
Axes of the slice: x: 4, y: 4 (y_hi: 2, y_lo: 2; y = y_hi * 2 + y_lo), z: 4, core: 2. Of those that a mesh axis runs over, the one named last changes fastest.
Arguments:
- matrix: float32 [16, 1024, 8, 2048], P(None, 'row', None, 'col'), may hold values from -150 to 150
- inverse_rest: float32 [16, 1024, 7, 2048], P(None, 'row', None, 'col'), may hold values from -6 to 6
- upper_block: float32 [2, 1024, 1, 2048], P(None, 'row', None, 'col'), may hold values from -6 to 6, as said below
- lower_below: float32 [2, 1024, 7, 2048], P(None, 'row', None, 'col'), may hold values from -0.046875 to 0.046875
- lower_inverse: float32 [2, 1024, 2048], P(None, 'row', 'col'), may hold values from -1 to 1, as said below
Outputs:
- plus_rows: float32 [2, 1024, 8, 2048], P(None, 'row', None, 'col')
Inputs may be any that keep to these rules, and one draw needn't show every extreme that they name: `upper_block`: upper triangular. `lower_inverse`: unit lower triangular.
All inputs are finite; a program needn't handle non-finite values.
Results may differ from a plain program's by a relative error of at most 0.000052.
Values sent between devices are 32-bit elements; how exact they have to be, the bound alone decides.
A program may use at most 192 MiB of HBM per device.

v0:
```python
import jax
import jax.numpy as jnp
from jax import lax
from jax.sharding import Mesh
from jax.sharding import PartitionSpec as P

ROW = ("row_0", "row_1")
COL = ("col_0", "col_1", "col_2")
ROW_COL = ("row_0", "row_1", "col_0", "col_1", "col_2")


def over_axes(array, axes):
    for axis in axes:
        array = lax.psum(array, axis)
    return array


def laid_out(pieces, dim):
    lengths = list(pieces.shape[1:])
    lengths[dim] *= pieces.shape[0]
    return jnp.moveaxis(pieces, 0, dim).reshape(lengths)


def from_everyone(array, axis):
    count = lax.axis_size(axis)
    return lax.all_to_all(
        jnp.broadcast_to(array[None], (count, *array.shape)), axis, 0, 0, tiled=True
    )


def collect(array, axis, dim):
    return laid_out(from_everyone(array, axis), dim)


def dot_exact(left, right, form):
    return jnp.einsum(
        form, left, right, precision=lax.Precision.HIGHEST, preferred_element_type=jnp.float32
    )


def mirror(panel_rows, row_devices, col_devices, panel_cycles, blk_size):
    share_rows, col_ratio, width_all = panel_rows.shape
    sectioned = panel_rows.reshape(share_rows, col_ratio, 1, panel_cycles, row_devices, blk_size)
    sectioned = lax.all_to_all(sectioned, ROW, split_axis=4, concat_axis=2, tiled=True)
    sectioned = sectioned.reshape(share_rows, col_devices, panel_cycles, blk_size)
    sectioned = lax.all_to_all(sectioned, COL, split_axis=1, concat_axis=0, tiled=True)
    return sectioned.reshape(col_devices * share_rows, panel_cycles * blk_size)


def per_device(matrix, inverse_rest, upper_block, lower_below, lower_inverse):
    row_devices = lax.axis_size(ROW)
    col_devices = lax.axis_size(COL)
    col_ratio = col_devices // row_devices
    row_cycles, blk_size, col_cycles, blk_again = matrix.shape
    panel_cycles = lower_inverse.shape[0]
    width_all = lower_inverse.shape[2] * col_devices
    rest_local = inverse_rest.shape[2] * blk_size
    panel_col_cycles = upper_block.shape[2]
    local_rows = col_cycles * blk_size
    share_rows = local_rows // col_devices
    matrix_sq = jnp.sum(matrix * matrix)
    rest_sq = jnp.sum(inverse_rest * inverse_rest)
    matrix_total, rest_total = (over_axes(matrix_sq, ROW_COL), over_axes(rest_sq, ROW_COL))
    below_all = lax.all_gather(lower_below, ROW, axis=1, tiled=True).reshape(width_all, rest_local)
    inverse_rows = (
        inverse_rest.reshape(col_cycles, col_ratio, blk_size, rest_local)
        .transpose(0, 2, 1, 3)
        .reshape(local_rows, col_ratio, rest_local)
    )
    padded = jnp.concatenate(
        [
            upper_block,
            jnp.zeros(
                (row_cycles - panel_cycles, blk_size, panel_col_cycles, blk_size), jnp.float32
            ),
        ],
        axis=0,
    )
    upper_rows = (
        padded.reshape(col_cycles, col_ratio, blk_size, panel_col_cycles * blk_size)
        .transpose(0, 2, 1, 3)
        .reshape(local_rows, col_ratio, panel_col_cycles, 1, blk_size)
    )
    owner_mask = lax.broadcasted_iota(jnp.int32, (1, 1, 1, col_devices, 1), 3) == lax.axis_index(
        COL
    )
    spread = jnp.where(owner_mask, upper_rows, 0.0).reshape(
        share_rows * lax.axis_size(COL), col_ratio, width_all
    )
    panel_share = lax.psum_scatter(
        spread - dot_exact(inverse_rows, below_all, "usm,tm->ust"),
        COL,
        scatter_dimension=0,
        tiled=True,
    )
    factor_rows = collect(lower_inverse, ROW, 1)
    factor_all = lax.all_gather(factor_rows, COL, axis=2, tiled=True).reshape(width_all, width_all)
    inverse_share = dot_exact(panel_share, factor_all, "ust,tw->usw")
    panel_sq = jnp.sum(inverse_share * inverse_share)
    mirrored = mirror(inverse_share, row_devices, col_devices, panel_cycles, blk_size)
    inverse_block = mirrored.reshape(col_cycles, blk_size, panel_cycles, blk_size).transpose(
        2, 3, 0, 1
    )
    panel_total = over_axes(panel_sq, ROW_COL)
    balance = jnp.sqrt(jnp.sqrt((rest_total + panel_total) / matrix_total))
    return 0.5 * (balance * matrix[:panel_cycles] + inverse_block / balance)


def solution(mesh):
    split = Mesh(mesh.devices.reshape(4, 2, 2, 4, 2), ("row_0", "row_1", "col_0", "col_1", "col_2"))
    return jax.shard_map(
        per_device,
        mesh=split,
        in_specs=(
            P(None, ROW, None, COL),
            P(None, ROW, None, COL),
            P(None, ROW, None, COL),
            P(None, ROW, None, COL),
            P(None, ROW, COL),
        ),
        out_specs=P(None, ROW, None, COL),
        check_vma=False,
    )
```

profile of v0, /device:TPU:1, one launch (start us, length us, event | category | flops | bytes accessed | tf_op | source)
XLA Modules:
  0.0 415.5 jit_solution(5951134886269617252)
XLA Ops:
  8.3 27.6 %all_to_all.29 = f32[8,2,128,128]{3,2,1,0:T(8,128)S(1)} all-to-all(f32[8,2,128,128]{3,2,1,0:T(8,128)S(1)} %broadcast_in_dim.42), channel_id=1, replica_groups=mesh['row_0'=4,'row_1'=2,'col_0'=2,'col_1'=4,'col_2'=2] {'row_0','row_1'}, dimensions={0} | all-to-all | bytes 2097152 | tf_op jit(solution)/shard_map/all_to_all | solution.py:26
  35.9 1.1 copy.41
  38.2 6.8 %broadcast_in_dim.39 = f32[1024,2,16,128]{3,2,0,1:T(8,128)} broadcast(f32[1024,2,128]{2,0,1:T(8,128)S(1)} %bitcast.51), dimensions={0,1,3} | broadcast | bytes 17825792 | tf_op jit(solution)/shard_map/jit(_where)/broadcast_in_dim | solution.py:87
  45.0 18.1 %broadcast_in_dim.40 = f32[1024,2,2048]{2,0,1:T(8,128)} reshape(f32[1024,2,16,128]{3,2,0,1:T(8,128)} %broadcast_in_dim.39) | data formatting | bytes 33554432 | tf_op jit(solution)/shard_map/jit(_where)/broadcast_in_dim | solution.py:87
  63.1 8.6 %copy.37 = f32[16,128,7,128]{1,3,2,0:T(8,128)} copy(f32[16,128,7,128]{3,1,2,0:T(8,128)} %param.6) | data formatting | bytes 14680064 | tf_op args[1]
  71.7 8.1 %copy.38 = f32[8,128,2,896]{3,1,0,2:T(8,128)} copy(f32[8,128,2,896]{1,3,2,0:T(8,128)} %bitcast.48) | data formatting | bytes 14680064 | tf_op jit(solution)/shard_map/transpose | solution.py:67
  79.9 33.9 %all-gather.3.cloned.1.call-done = f32[2,1024,7,128]{3,1,2,0:T(8,128)} async-done(((f32[2,128,7,128]{3,1,2,0:T(8,128)}), f32[2,1024,7,128]{3,1,2,0:T(8,128)}) %all-gather.3.cloned.1.call-update) | async-done | bytes 7340048 | tf_op jit(solution)/shard_map/all_gather | solution.py:64
  113.8 11.8 %copy.39 = f32[2,1024,7,128]{1,0,3,2:T(2,128)} copy(f32[2,1024,7,128]{3,1,2,0:T(8,128)} %all-gather.3.cloned.1.call-done) | data formatting | bytes 14680064 | tf_op jit(solution)/shard_map/all_gather | solution.py:64
  125.6 10.7 %reshape.58 = f32[2048,896,1]{0,1,2:T(8,128)} reshape(f32[2,1024,7,128]{1,0,3,2:T(2,128)} %copy.39) | data formatting | bytes 14680064 | tf_op jit(solution)/shard_map/reshape | solution.py:64
  136.3 60.3 %select_subtract_fusion = f32[1024,2,2048]{2,0,1:T(8,128)} fusion(f32[1024,2,2048]{2,0,1:T(8,128)} %broadcast_in_dim.40, pred[2048]{0:T(1024)(128)(4,1)S(1)} %broadcast_bitcast_fusion, f32[1024,2,896]{2,0,1:T(8,128)} %bitcast.49, f32[2048,896,1]{0,1,2:T(8,128)} %reshape.58), kind=kOutput, calls=%fused_computation | convolution fusion | flops 45105545216 | bytes 48236544 | tf_op jit(solution)/shard_map/usm,tm->ust/dot_general | solution.py:36
  196.6 15.5 %all-gather.5.cloned.1.call-done = f32[2,1024,2048]{2,1,0:T(8,128)} async-done(((f32[2,1024,128]{2,1,0:T(8,128)}), f32[2,1024,2048]{2,1,0:T(8,128)}) %all-gather.5.cloned.1.call-update) | async-done | bytes 16777232 | tf_op jit(solution)/shard_map/all_gather | solution.py:97
  212.1 98.9 %reduce-scatter.2.cloned.1.call-done = f32[64,2,2048]{2,0,1:T(8,128)} async-done(((f32[1024,2,2048]{2,0,1:T(8,128)}), f32[64,2,2048]{2,0,1:T(8,128)}) %reduce-scatter.2.cloned.1.call-update) | async-done | bytes 1048592 | tf_op jit(solution)/shard_map/reduce_scatter | solution.py:90
  310.9 13.6 %multiply_reduce_fusion.2 = (f32[]{:T(128)}, f32[64,2,2048]{2,0,1:T(8,128)S(1)}) fusion(f32[64,2,2048]{2,0,1:T(8,128)} %reduce-scatter.2.cloned.1.call-done, f32[2048,2048,1]{1,0,2:T(8,128)} %bitcast.47), kind=kOutput, calls=%fused_computation.6 | convolution fusion | flops 6442975232 | bytes 18874372 | tf_op jit(solution)/shard_map/ust,tw->usw/dot_general | solution.py:36
  325.5 21.3 %all_to_all.30 = f32[64,2,1,2,8,128]{5,1,3,0,2,4:T(2,128)S(1)} all-to-all(f32[64,2,1,2,8,128]{5,1,3,0,2,4:T(2,128)S(1)} %copy.43), channel_id=1, replica_groups=mesh['row_0'=4,'row_1'=2,'col_0'=2,'col_1'=4,'col_2'=2] {'row_0','row_1'}, dimensions={4} | all-to-all | bytes 2097152 | tf_op jit(solution)/shard_map/all_to_all | solution.py:44
  347.5 1.5 copy.45
  349.0 7.3 %all-to-all-start.2 = ((f32[64,16,2,128]{3,2,0,1:T(2,128)}), f32[64,16,2,128]{3,2,0,1:T(2,128)S(1)}, u32[]{:S(2)}, u32[]{:S(2)}) async-start(f32[64,16,2,128]{3,2,0,1:T(2,128)} %copy.45), calls=%async_computation.3 | async-start | bytes 2097152 | tf_op jit(solution)/shard_map/all_to_all | solution.py:46
  356.3 5.7 %multiply_reduce_fusion.1 = f32[]{:T(128)} fusion(f32[16,128,7,128]{3,1,2,0:T(8,128)} %param.6), kind=kLoop, calls=%fused_computation.2 | loop fusion | flops 3670015 | bytes 7340036 | tf_op jit(solution)/shard_map/reduce_sum | solution.py:62
  361.9 6.2 %multiply_reduce_fusion = f32[]{:T(128)} fusion(f32[16,128,8,128]{3,2,1,0:T(8,128)} %param.5), kind=kLoop, calls=%fused_computation.1 | loop fusion | flops 4194303 | bytes 8388612 | tf_op jit(solution)/shard_map/reduce_sum | solution.py:61
  369.7 7.1 %all-reduce.2 = (f32[]{:T(128)}, f32[]{:T(128)}) all-reduce(f32[]{:T(128)S(6)} %add.48, f32[]{:T(128)} %multiply_reduce_fusion), channel_id=1, replica_groups=mesh['row_0'=4,'row_1'=2,'col_0'=2,'col_1'=4,'col_2'=2] {'row_0'}, use_global_device_ids=true, to_apply=%region_1.0 | all-reduce | flops 2 | bytes 16 | tf_op jit(solution)/shard_map/psum | solution.py:14
  376.7 5.9 %all-reduce.5 = (f32[]{:T(128)}, f32[]{:T(128)}) all-reduce(f32[]{:T(128)} %get-tuple-element.7, f32[]{:T(128)} %get-tuple-element.8), channel_id=1, replica_groups=mesh['row_0'=4,'row_1'=2,'col_0'=2,'col_1'=4,'col_2'=2] {'row_1'}, use_global_device_ids=true, to_apply=%region_2.0 | all-reduce | flops 2 | bytes 16 | tf_op jit(solution)/shard_map/psum | solution.py:14
  382.7 4.5 %all-reduce.4 = (f32[]{:T(128)}, f32[]{:T(128)}) all-reduce(f32[]{:T(128)} %get-tuple-element.13, f32[]{:T(128)} %get-tuple-element.14), channel_id=1, replica_groups=mesh['row_0'=4,'row_1'=2,'col_0'=2,'col_1'=4,'col_2'=2] {'col_0'}, use_global_device_ids=true, to_apply=%region_3.0 | all-reduce | flops 2 | bytes 16 | tf_op jit(solution)/shard_map/psum | solution.py:14
  387.1 9.2 %all-reduce.1 = (f32[]{:T(128)}, f32[]{:T(128)}) all-reduce(f32[]{:T(128)} %get-tuple-element.11, f32[]{:T(128)} %get-tuple-element.12), channel_id=1, replica_groups=mesh['row_0'=4,'row_1'=2,'col_0'=2,'col_1'=4,'col_2'=2] {'col_1'}, use_global_device_ids=true, to_apply=%region_4.0 | all-reduce | flops 2 | bytes 16 | tf_op jit(solution)/shard_map/psum | solution.py:14
  396.3 9.6 %all-reduce.3 = (f32[]{:T(128)}, f32[]{:T(128)}) all-reduce(f32[]{:T(128)} %get-tuple-element.5, f32[]{:T(128)} %get-tuple-element.6), channel_id=1, replica_groups=mesh['row_0'=4,'row_1'=2,'col_0'=2,'col_1'=4,'col_2'=2] {'col_2'}, use_global_device_ids=true, to_apply=%region_5.0 | all-reduce | flops 2 | bytes 16 | tf_op jit(solution)/shard_map/psum | solution.py:14
  407.6 1.3 copy.47
  (20 shorter events, 5.3 us)
Async XLA Ops:
  6.5 107.3 %all-gather.3.cloned.1.call-start = ((), (), s32[]{:S(2)}) async-start(), calls=%async_computation.4 | async-start | bytes 8257536 | tf_op jit(solution)/shard_map/all_gather | solution.py:64
  7.3 204.8 %all-gather.5.cloned.1.call-start = ((), (), s32[]{:S(2)}) async-start(), calls=%async_computation.6 | async-start | bytes 17825792 | tf_op jit(solution)/shard_map/all_gather | solution.py:97
  37.0 273.9 %reduce-scatter.2.cloned.1.call-start = ((), (), s32[]{:S(2)}) async-start(), calls=%async_computation.5 | async-start | bytes 17825792 | tf_op jit(solution)/shard_map/reduce_scatter | solution.py:90
  349.0 58.4 %all-to-all-start.2 = ((f32[64,16,2,128]{3,2,0,1:T(2,128)}), f32[64,16,2,128]{3,2,0,1:T(2,128)S(1)}, u32[]{:S(2)}, u32[]{:S(2)}) async-start(f32[64,16,2,128]{3,2,0,1:T(2,128)} %copy.45), calls=%async_computation.3 | async-start | bytes 2097152 | tf_op jit(solution)/shard_map/all_to_all | solution.py:46
  356.3 13.0 %slice-start = ((f32[16,128,8,128]{3,2,1,0:T(8,128)}), f32[2,128,8,128]{3,2,1,0:T(8,128)S(1)}, s32[]{:S(2)}) async-start(f32[16,128,8,128]{3,2,1,0:T(8,128)} %param.5), calls=%async_computation.7 | async-start | bytes 2097152 | tf_op jit(solution)/shard_map/slice | solution.py:106
Sparse Core Ops, SparseCore 0:
  9.6 104.1 all-gather.2
  115.4 96.6 all-gather.4
  214.5 96.4 reduce-scatter.1
where the time goes:
time: 417 us; the launch traced here: 415 us
  waiting for transfers between devices  149 us (36%)
  blocking collectives  85.1 us (20%)
  matrix products  73.9 us (18%)
  local copies, waits for them, and re-layouts  72.2 us (17%)
  between operations  15.8 us (4%)
  other arithmetic  12.2 us (3%)
  starting transfers between devices  7.39 us (2%)
    reduce_scatter x1, waiting for transfers between devices, per_device(): lax.psum_scatter(spread - dot_exact(inverse_rows, below_all, 'usm,tm->ust...  98.9 us
    dot_general x2, matrix products, dot_exact(): jnp.einsum(form, left, right, precision=lax.Precision.HIGHEST, preferred_...  73.9 us
    psum x5, blocking collectives, over_axes(): array = lax.psum(array, axis)  36.2 us
    all_gather x1, waiting for transfers between devices, per_device(): lax.all_gather(lower_below, ROW, axis=1, tiled=True)  33.9 us
    all_to_all x1, blocking collectives, from_everyone(): lax.all_to_all(jnp.broadcast_to(array[None], (count, *array.shape)), axis...  27.6 us
    broadcast_in_dim x3, local copies, waits for them, and re-layouts, per_device(): jnp.where(owner_mask, upper_rows, 0.0)  25 us
    all_to_all x1, blocking collectives, mirror(): lax.all_to_all(sectioned, ROW, split_axis=4, concat_axis=2, tiled=True)  21.3 us
    all_gather x1, waiting for transfers between devices, per_device(): lax.all_gather(factor_rows, COL, axis=2, tiled=True)  15.5 us
  transfers between devices with their start and end apart: 4, of which 3 were waited for; matrix products, arithmetic and copies ran while one was open for 34% of the time, Pallas kernels for 0%

commit v1 on v0

--- a/solution.py
+++ b/solution.py
@@ -7,6 +7,14 @@
 ROW = ("row_0", "row_1")
 COL = ("col_0", "col_1", "col_2")
 ROW_COL = ("row_0", "row_1", "col_0", "col_1", "col_2")
+
+
+def target_recover(a0):
+    pool = []
+    for _ in range(lax.axis_size(ROW)):
+        pool.append(a0)
+    oldest = lax.all_to_all(jnp.stack(pool, axis=0), ROW, 0, 0)
+    return jnp.concatenate(oldest, axis=1)
 
 
 def over_axes(array, axes):
@@ -61,7 +69,7 @@
     matrix_sq = jnp.sum(matrix * matrix)
     rest_sq = jnp.sum(inverse_rest * inverse_rest)
     matrix_total, rest_total = (over_axes(matrix_sq, ROW_COL), over_axes(rest_sq, ROW_COL))
-    below_all = lax.all_gather(lower_below, ROW, axis=1, tiled=True).reshape(width_all, rest_local)
+    below_all = target_recover(lower_below).reshape(width_all, rest_local)
     inverse_rows = (
         inverse_rest.reshape(col_cycles, col_ratio, blk_size, rest_local)
         .transpose(0, 2, 1, 3)

time: 417 us -> 483 us (1.16)
  waiting for transfers between devices: 149 us -> 209 us
  starting transfers between devices: 7.39 us -> 12.3 us
    all_to_all x0 -> x1, waiting for transfers between devices: none -> 115 us  [target_recover(): oldest = lax.all_to_all(jnp.stack(pool, axis=0), ROW, 0, 0)]
    all_gather x1 -> x0, waiting for transfers between devices: 33.9 us -> none  [per_device(): lax.all_gather(lower_below, ROW, axis=1, tiled=True)]
    another operation x0 -> x2, local copies, waits for them, and re-layouts: none -> 15.5 us  [the longest x1 8.96 us: per_device(): below_all = target_recover(lower_below).reshape(width_all, rest_local)]
    all_gather x1, waiting for transfers between devices: 15.5 us -> 0.02 us  [per_device(): lax.all_gather(factor_rows, COL, axis=2, tiled=True)]
    all_gather x1 -> x0, local copies, waits for them, and re-layouts: 11.8 us -> none  [per_device(): lax.all_gather(lower_below, ROW, axis=1, tiled=True)]
    all_to_all x0 -> x1, starting transfers between devices: none -> 5 us  [target_recover(): oldest = lax.all_to_all(jnp.stack(pool, axis=0), ROW, 0, 0)]
    unnamed x3 -> x6, local copies, waits for them, and re-layouts: 9.15 us -> 11 us
  transfers between devices with their start and end apart: 4 -> 4, of which waited for: 3 -> 2; matrix products, arithmetic and copies ran while one was open for 34% -> 29% of each run, Pallas kernels for 0% -> 0%
where the time goes in v1:
time: 483 us; the launch traced here: 482 us
  waiting for transfers between devices  209 us (43%)
  blocking collectives  82.2 us (17%)
  local copies, waits for them, and re-layouts  76.4 us (16%)
  matrix products  73.3 us (15%)
  between operations  16.2 us (3%)
  starting transfers between devices  12.3 us (3%)
  other arithmetic  12.2 us (3%)
    all_to_all x1, waiting for transfers between devices, target_recover(): oldest = lax.all_to_all(jnp.stack(pool, axis=0), ROW, 0, 0)  115 us
    reduce_scatter x1, waiting for transfers between devices, per_device(): lax.psum_scatter(spread - dot_exact(inverse_rows, below_all, 'usm,tm->ust...  94.1 us
    dot_general x2, matrix products, dot_exact(): jnp.einsum(form, left, right, precision=lax.Precision.HIGHEST, preferred_...  73.3 us
    psum x5, blocking collectives, over_axes(): array = lax.psum(array, axis)  36.3 us
    broadcast_in_dim x3, local copies, waits for them, and re-layouts, per_device(): jnp.where(owner_mask, upper_rows, 0.0)  24.9 us
    all_to_all x1, blocking collectives, from_everyone(): lax.all_to_all(jnp.broadcast_to(array[None], (count, *array.shape)), axis...  24.6 us
    all_to_all x1, blocking collectives, mirror(): lax.all_to_all(sectioned, ROW, split_axis=4, concat_axis=2, tiled=True)  21.3 us
    unnamed x6, local copies, waits for them, and re-layouts  11 us
  transfers between devices with their start and end apart: 4, of which 2 were waited for; matrix products, arithmetic and copies ran while one was open for 29% of the time, Pallas kernels for 0%

profile of v1, /device:TPU:1, one launch (start us, length us, event | category | flops | bytes accessed | tf_op | source)
XLA Modules:
  0.0 481.9 jit_solution(2821169025570760894)
XLA Ops:
  7.5 24.6 %all_to_all.34 = f32[8,2,128,128]{3,2,1,0:T(8,128)S(1)} all-to-all(f32[8,2,128,128]{3,2,1,0:T(8,128)S(1)} %broadcast_in_dim.42), channel_id=1, replica_groups=mesh['row_0'=4,'row_1'=2,'col_0'=2,'col_1'=4,'col_2'=2] {'row_0','row_1'}, dimensions={0} | all-to-all | bytes 2097152 | tf_op jit(solution)/shard_map/all_to_all | solution.py:34
  33.3 1.9 copy.41
  35.1 6.5 %stack.2 = f32[8,2,128,7,128]{2,1,4,3,0:T(2,128)} broadcast(f32[2,128,7,128]{1,0,3,2:T(2,128)S(1)} %copy.41), dimensions={1,2,3,4} | broadcast | bytes 8257536 | tf_op jit(solution)/shard_map/stack | solution.py:16
  41.7 5.0 %all-to-all-start = ((f32[8,2,128,7,128]{2,1,4,3,0:T(2,128)}), f32[8,2,128,7,128]{2,1,4,3,0:T(2,128)}, u32[]{:S(2)}, u32[]{:S(2)}) async-start(f32[8,2,128,7,128]{2,1,4,3,0:T(2,128)} %stack.2), calls=%async_computation | async-start | bytes 14680064 | tf_op jit(solution)/shard_map/all_to_all | solution.py:16
  47.0 6.8 %broadcast_in_dim.39 = f32[1024,2,16,128]{3,2,0,1:T(8,128)} broadcast(f32[1024,2,128]{2,0,1:T(8,128)S(1)} %bitcast.54), dimensions={0,1,3} | broadcast | bytes 17825792 | tf_op jit(solution)/shard_map/jit(_where)/broadcast_in_dim | solution.py:95
  53.7 18.1 %broadcast_in_dim.40 = f32[1024,2,2048]{2,0,1:T(8,128)} reshape(f32[1024,2,16,128]{3,2,0,1:T(8,128)} %broadcast_in_dim.39) | data formatting | bytes 33554432 | tf_op jit(solution)/shard_map/jit(_where)/broadcast_in_dim | solution.py:95
  71.8 8.6 %copy.39 = f32[16,128,7,128]{1,3,2,0:T(8,128)} copy(f32[16,128,7,128]{3,1,2,0:T(8,128)} %param.6) | data formatting | bytes 14680064 | tf_op args[1]
  80.4 8.2 %copy.40 = f32[8,128,2,896]{3,1,0,2:T(8,128)} copy(f32[8,128,2,896]{1,3,2,0:T(8,128)} %bitcast.51) | data formatting | bytes 14680064 | tf_op jit(solution)/shard_map/transpose | solution.py:75
  88.7 115.1 %all-to-all-done = f32[8,2,128,7,128]{2,1,4,3,0:T(2,128)} async-done(((f32[8,2,128,7,128]{2,1,4,3,0:T(2,128)}), f32[8,2,128,7,128]{2,1,4,3,0:T(2,128)}, u32[]{:S(2)}, u32[]{:S(2)}) %all-to-all-start) | async-done | bytes 7340064 | tf_op jit(solution)/shard_map/all_to_all | solution.py:16
  203.8 10.2 %copy.42 = f32[2,8,128,7,128]{2,1,0,4,3:T(8,128)} copy(f32[2,8,128,7,128]{2,0,4,3,1:T(2,128)} %bitcast.8) | data formatting | bytes 14680064 | tf_op jit(solution)/shard_map/reshape | solution.py:17
  214.0 9.0 %reshape.60 = f32[2048,896,1]{0,1,2:T(8,128)} reshape(f32[2,8,128,7,128]{2,1,0,4,3:T(8,128)} %copy.42) | data formatting | bytes 14680064 | tf_op jit(solution)/shard_map/reshape;reshape | solution.py:72
  223.0 59.7 %select_subtract_fusion = f32[1024,2,2048]{2,0,1:T(8,128)} fusion(f32[1024,2,2048]{2,0,1:T(8,128)} %broadcast_in_dim.40, pred[2048]{0:T(1024)(128)(4,1)S(1)} %broadcast_bitcast_fusion, f32[1024,2,896]{2,0,1:T(8,128)} %bitcast.52, f32[2048,896,1]{0,1,2:T(8,128)} %reshape.60), kind=kOutput, calls=%fused_computation | convolution fusion | flops 45105545216 | bytes 48236544 | tf_op jit(solution)/shard_map/usm,tm->ust/dot_general | solution.py:44
  282.8 94.1 %reduce-scatter.2.cloned.1.call-done = f32[64,2,2048]{2,0,1:T(8,128)} async-done(((f32[1024,2,2048]{2,0,1:T(8,128)}), f32[64,2,2048]{2,0,1:T(8,128)}) %reduce-scatter.2.cloned.1.call-update) | async-done | bytes 1048592 | tf_op jit(solution)/shard_map/reduce_scatter | solution.py:98
  376.9 13.6 %multiply_reduce_fusion.2 = (f32[]{:T(128)}, f32[64,2,2048]{2,0,1:T(8,128)S(1)}) fusion(f32[64,2,2048]{2,0,1:T(8,128)} %reduce-scatter.2.cloned.1.call-done, f32[2048,2048,1]{1,0,2:T(8,128)} %bitcast.50), kind=kOutput, calls=%fused_computation.6 | convolution fusion | flops 6442975232 | bytes 18874372 | tf_op jit(solution)/shard_map/ust,tw->usw/dot_general | solution.py:44
  391.5 21.3 %all_to_all.35 = f32[64,2,1,2,8,128]{5,1,3,0,2,4:T(2,128)S(1)} all-to-all(f32[64,2,1,2,8,128]{5,1,3,0,2,4:T(2,128)S(1)} %copy.46), channel_id=1, replica_groups=mesh['row_0'=4,'row_1'=2,'col_0'=2,'col_1'=4,'col_2'=2] {'row_0','row_1'}, dimensions={4} | all-to-all | bytes 2097152 | tf_op jit(solution)/shard_map/all_to_all | solution.py:52
  413.4 1.5 copy.48
  414.9 7.3 %all-to-all-start.3 = ((f32[64,16,2,128]{3,2,0,1:T(2,128)}), f32[64,16,2,128]{3,2,0,1:T(2,128)S(1)}, u32[]{:S(2)}, u32[]{:S(2)}) async-start(f32[64,16,2,128]{3,2,0,1:T(2,128)} %copy.48), calls=%async_computation.4 | async-start | bytes 2097152 | tf_op jit(solution)/shard_map/all_to_all | solution.py:54
  422.3 5.7 %multiply_reduce_fusion.1 = f32[]{:T(128)} fusion(f32[16,128,7,128]{3,1,2,0:T(8,128)} %param.6), kind=kLoop, calls=%fused_computation.2 | loop fusion | flops 3670015 | bytes 7340036 | tf_op jit(solution)/shard_map/reduce_sum | solution.py:70
  428.0 6.2 %multiply_reduce_fusion = f32[]{:T(128)} fusion(f32[16,128,8,128]{3,2,1,0:T(8,128)} %param.5), kind=kLoop, calls=%fused_computation.1 | loop fusion | flops 4194303 | bytes 8388612 | tf_op jit(solution)/shard_map/reduce_sum | solution.py:69
  435.8 7.1 %all-reduce.2 = (f32[]{:T(128)}, f32[]{:T(128)}) all-reduce(f32[]{:T(128)S(6)} %add.48, f32[]{:T(128)} %multiply_reduce_fusion), channel_id=1, replica_groups=mesh['row_0'=4,'row_1'=2,'col_0'=2,'col_1'=4,'col_2'=2] {'row_0'}, use_global_device_ids=true, to_apply=%region_1.0 | all-reduce | flops 2 | bytes 16 | tf_op jit(solution)/shard_map/psum | solution.py:22
  442.9 6.0 %all-reduce.5 = (f32[]{:T(128)}, f32[]{:T(128)}) all-reduce(f32[]{:T(128)} %get-tuple-element.7, f32[]{:T(128)} %get-tuple-element.8), channel_id=1, replica_groups=mesh['row_0'=4,'row_1'=2,'col_0'=2,'col_1'=4,'col_2'=2] {'row_1'}, use_global_device_ids=true, to_apply=%region_2.0 | all-reduce | flops 2 | bytes 16 | tf_op jit(solution)/shard_map/psum | solution.py:22
  448.9 4.5 all-reduce.4
  453.3 9.2 %all-reduce.1 = (f32[]{:T(128)}, f32[]{:T(128)}) all-reduce(f32[]{:T(128)} %get-tuple-element.11, f32[]{:T(128)} %get-tuple-element.12), channel_id=1, replica_groups=mesh['row_0'=4,'row_1'=2,'col_0'=2,'col_1'=4,'col_2'=2] {'col_1'}, use_global_device_ids=true, to_apply=%region_4.0 | all-reduce | flops 2 | bytes 16 | tf_op jit(solution)/shard_map/psum | solution.py:22
  462.6 9.5 %all-reduce.3 = (f32[]{:T(128)}, f32[]{:T(128)}) all-reduce(f32[]{:T(128)} %get-tuple-element.5, f32[]{:T(128)} %get-tuple-element.6), channel_id=1, replica_groups=mesh['row_0'=4,'row_1'=2,'col_0'=2,'col_1'=4,'col_2'=2] {'col_2'}, use_global_device_ids=true, to_apply=%region_5.0 | all-reduce | flops 2 | bytes 16 | tf_op jit(solution)/shard_map/psum | solution.py:22
  (23 shorter events, 6.0 us)
Async XLA Ops:
  6.5 276.2 %all-gather.2.cloned.1.call-start = ((), (), s32[]{:S(2)}) async-start(), calls=%async_computation.6 | async-start | bytes 17825792 | tf_op jit(solution)/shard_map/all_gather | solution.py:105
  41.7 5.1 %copy-start = (f32[2,128,1,128]{3,2,1,0:T(1,128)S(1)}, f32[2,128,1,128]{3,2,1,0:T(1,128)}, u32[]{:S(2)}) copy-start(f32[2,128,1,128]{3,2,1,0:T(1,128)} %param.7) | copy-start | bytes 393220
  41.7 162.1 %all-to-all-start = ((f32[8,2,128,7,128]{2,1,4,3,0:T(2,128)}), f32[8,2,128,7,128]{2,1,4,3,0:T(2,128)}, u32[]{:S(2)}, u32[]{:S(2)}) async-start(f32[8,2,128,7,128]{2,1,4,3,0:T(2,128)} %stack.2), calls=%async_computation | async-start | bytes 14680064 | tf_op jit(solution)/shard_map/all_to_all | solution.py:16
  46.7 330.2 %reduce-scatter.2.cloned.1.call-start = ((), (), s32[]{:S(2)}) async-start(), calls=%async_computation.5 | async-start | bytes 17825792 | tf_op jit(solution)/shard_map/reduce_scatter | solution.py:98
  414.9 58.6 %all-to-all-start.3 = ((f32[64,16,2,128]{3,2,0,1:T(2,128)}), f32[64,16,2,128]{3,2,0,1:T(2,128)S(1)}, u32[]{:S(2)}, u32[]{:S(2)}) async-start(f32[64,16,2,128]{3,2,0,1:T(2,128)} %copy.48), calls=%async_computation.4 | async-start | bytes 2097152 | tf_op jit(solution)/shard_map/all_to_all | solution.py:54
  422.2 13.2 %slice-start = ((f32[16,128,8,128]{3,2,1,0:T(8,128)}), f32[2,128,8,128]{3,2,1,0:T(8,128)S(1)}, s32[]{:S(2)}) async-start(f32[16,128,8,128]{3,2,1,0:T(8,128)} %param.5), calls=%async_computation.7 | async-start | bytes 2097152 | tf_op jit(solution)/shard_map/slice | solution.py:114
Sparse Core Ops, SparseCore 0:
  33.4 164.4 all-gather.1
  282.9 93.9 reduce-scatter.1
